TPU v7x, 32 devices: a whole 2x2x4 slice. The times are simulated.
32 devices in a mesh: dp: 8 (over y, x, core), mp: 4 (over z).
Axes of the slice: x: 2, y: 2, z: 4, core: 2. Of those that a mesh axis runs over, the one named last changes fastest.
Arguments:
- tokens: bfloat16 [512, 8192], P('mp', 'dp'), may hold values from -6 to 6
- cotangent: bfloat16 [512, 8192], P('mp', 'dp'), may hold values from -1.5 to 1.5
- gate_weight: bfloat16 [8192, 14336], P('dp', 'mp'), may hold values from -0.0625 to 0.0625
- up_weight: bfloat16 [8192, 14336], P('dp', 'mp'), may hold values from -0.0625 to 0.0625
- down_weight: bfloat16 [14336, 8192], P('mp', 'dp'), may hold values from -0.046875 to 0.046875
Outputs:
- output: bfloat16 [512, 8192], P('mp', 'dp')
- grad_input: bfloat16 [512, 8192], P('mp', 'dp')
- grad_gate: bfloat16 [8192, 14336], P('dp', 'mp')
- grad_up: bfloat16 [8192, 14336], P('dp', 'mp')
- grad_down: bfloat16 [14336, 8192], P('mp', 'dp')
All inputs are finite; a program needn't handle non-finite values.
Results may differ from a plain program's by a relative error of at most 0.013.
Values may be sent and summed in bfloat16 or wider, within the bound.
No kernel may reach another device: no remote copies, remote signals or barrier semaphores. Data moves between devices by JAX's collectives and lax.ppermute only.
A program may use at most 128 MiB of HBM per device.

v0:
```python
import jax
import jax.numpy as jnp
from jax import lax
from jax.sharding import PartitionSpec as P


def contract(left, right, left_dim, right_dim):
    return lax.dot_general(
        left, right, (((left_dim,), (right_dim,)), ((), ())), preferred_element_type=jnp.float32
    )


def per_device(tokens, cotangent, gate_weight, up_weight, down_weight):
    all_tokens, all_cotangent = (
        lax.all_gather(tokens, "mp", axis=0, tiled=True),
        lax.all_gather(cotangent, "mp", axis=0, tiled=True),
    )
    columns = gate_weight.shape[1]
    rows = all_tokens
    stacked = lax.psum_scatter(
        jnp.concatenate(
            [
                jnp.dot(rows, gate_weight, preferred_element_type=jnp.float32),
                jnp.dot(rows, up_weight, preferred_element_type=jnp.float32),
            ],
            axis=1,
        ),
        "dp",
        scatter_dimension=0,
        tiled=True,
    )
    gate = stacked[:, :columns]
    up = stacked[:, columns:]
    sig = jax.nn.sigmoid(gate)
    hidden = (gate * sig * up).astype(jnp.bfloat16)
    all_hidden = lax.all_gather(hidden, "dp", axis=0, tiled=True)
    rows = all_hidden
    output = lax.psum_scatter(
        jnp.dot(rows, down_weight, preferred_element_type=jnp.float32).astype(jnp.bfloat16),
        "mp",
        scatter_dimension=0,
        tiled=True,
    )
    grad_down = contract(all_hidden, all_cotangent, 0, 0).astype(jnp.bfloat16)
    rows = all_cotangent
    d_hidden = lax.psum_scatter(
        contract(rows, down_weight, 1, 1), "dp", scatter_dimension=0, tiled=True
    )
    d_gate = (d_hidden * up * sig * (1.0 + gate * (1.0 - sig))).astype(jnp.bfloat16)
    d_up = (d_hidden * gate * sig).astype(jnp.bfloat16)
    all_d_gate, all_d_up = (
        lax.all_gather(d_gate, "dp", axis=0, tiled=True),
        lax.all_gather(d_up, "dp", axis=0, tiled=True),
    )
    grad_gate = contract(all_tokens, all_d_gate, 0, 0).astype(jnp.bfloat16)
    grad_up = contract(all_tokens, all_d_up, 0, 0).astype(jnp.bfloat16)
    grad_input = lax.psum_scatter(
        (contract(all_d_gate, gate_weight, 1, 1) + contract(all_d_up, up_weight, 1, 1)).astype(
            jnp.bfloat16
        ),
        "mp",
        scatter_dimension=0,
        tiled=True,
    )
    return (output, grad_input, grad_gate, grad_up, grad_down)


def solution(mesh):
    placed = (P("mp", "dp"), P("mp", "dp"), P("dp", "mp"), P("dp", "mp"), P("mp", "dp"))
    return jax.shard_map(
        per_device,
        mesh=mesh,
        in_specs=placed,
        out_specs=(P("mp", "dp"), P("mp", "dp"), P("dp", "mp"), P("dp", "mp"), P("mp", "dp")),
        check_vma=False,
    )
```

profile of v0, /device:TPU:0, one launch (start us, length us, event | category | flops | bytes accessed | tf_op | source)
XLA Modules:
  0.0 424.4 jit_solution(3029264662274093701)
XLA Ops:
  7.2 0.0 all-gather.10.cloned.1.call-start
  7.2 0.7 all-gather.10.cloned.1.call-update
  7.9 0.0 all-gather.6.cloned.1.call-start
  7.9 0.7 all-gather.6.cloned.1.call-update
  8.6 0.0 reduce-scatter.9.cloned.1.call-start
  8.7 31.6 %all-gather.10.cloned.1.call-done = bf16[512,1024]{1,0:T(8,128)(2,1)} async-done(((bf16[128,1024]{1,0:T(8,128)(2,1)}), bf16[512,1024]{1,0:T(8,128)(2,1)}) %all-gather.10.cloned.1.call-update) | async-done | bytes 1048592 | tf_op jit(solution)/shard_map/all_gather | solution.py:16
  40.3 10.5 %fusion.4 = f32[512,3584]{1,0:T(8,128)} fusion(bf16[512,1024]{1,0:T(8,128)(2,1)} %all-gather.10.cloned.1.call-done, bf16[3584,1024]{1,0:T(8,128)(2,1)} %param.9), kind=kOutput, calls=%fused_computation.14 | convolution fusion | flops 3758096384 | bytes 15728640 | tf_op jit(solution)/shard_map/dot_general | solution.py:8
  50.7 0.0 reduce-scatter.9.cloned.1.call-update
  50.8 0.0 reduce-scatter.5.cloned.1.call-start
  50.8 18.4 %all-gather.6.cloned.1.call-done = bf16[512,1024]{1,0:T(8,128)(2,1)} async-done(((bf16[128,1024]{1,0:T(8,128)(2,1)}), bf16[512,1024]{1,0:T(8,128)(2,1)}) %all-gather.6.cloned.1.call-update) | async-done | bytes 1048592 | tf_op jit(solution)/shard_map/all_gather | solution.py:15
  69.2 0.0 copy-start.1
  69.2 7.4 %fusion.2 = f32[512,3584]{1,0:T(8,128)S(1)} fusion(bf16[512,1024]{1,0:T(8,128)(2,1)} %all-gather.6.cloned.1.call-done, bf16[1024,3584]{1,0:T(8,128)(2,1)} %param.7), kind=kOutput, calls=%fused_computation.12 | convolution fusion | flops 3758096384 | bytes 15728640 | tf_op jit(solution)/shard_map/dot_general | solution.py:23
  76.7 0.0 copy-done.1
  76.7 6.8 %fusion.3 = f32[512,3584]{1,0:T(8,128)S(1)} fusion(bf16[512,1024]{1,0:T(8,128)(2,1)S(1)} %copy-done.1, bf16[1024,3584]{1,0:T(8,128)(2,1)} %param.8), kind=kOutput, calls=%fused_computation.13 | convolution fusion | flops 3758096384 | bytes 15728640 | tf_op jit(solution)/shard_map/dot_general | solution.py:24
  83.5 6.4 %pad_maximum_fusion = f32[512,7168]{1,0:T(8,128)} fusion(f32[512,3584]{1,0:T(8,128)S(1)} %fusion.3, f32[512,3584]{1,0:T(8,128)S(1)} %fusion.2), kind=kLoop, calls=%fused_computation | loop fusion | flops 3670016 | bytes 29360128 | tf_op jit(solution)/shard_map/concatenate | solution.py:21
  89.9 0.0 reduce-scatter.5.cloned.1.call-update
  89.9 0.0 all-gather.12.cloned.1.call-start
  90.0 49.6 %reduce-scatter.9.cloned.1.call-done = f32[64,3584]{1,0:T(8,128)} async-done(((f32[512,3584]{1,0:T(8,128)}), f32[64,3584]{1,0:T(8,128)}) %reduce-scatter.9.cloned.1.call-update) | async-done | bytes 917520 | tf_op jit(solution)/shard_map/reduce_scatter | solution.py:46
  139.6 108.0 %reduce-scatter.5.cloned.1.call-done = f32[64,7168]{1,0:T(8,128)} async-done(((f32[512,7168]{1,0:T(8,128)}), f32[64,7168]{1,0:T(8,128)}) %reduce-scatter.5.cloned.1.call-update) | async-done | bytes 1835024 | tf_op jit(solution)/shard_map/reduce_scatter | solution.py:20
  247.6 3.2 multiply_convert_fusion
  250.8 0.0 all-gather.12.cloned.1.call-update
  250.8 0.0 all-gather.14.cloned.1.call-start
  250.9 0.5 all-gather.14.cloned.1.call-update
  251.4 0.0 all-gather.8.cloned.1.call-start
  251.5 0.7 all-gather.8.cloned.1.call-update
  252.2 0.0 reduce-scatter.11.cloned.1.call-start
  252.2 33.2 %all-gather.12.cloned.1.call-done = bf16[512,3584]{1,0:T(8,128)(2,1)} async-done(((bf16[64,3584]{1,0:T(8,128)(2,1)}), bf16[512,3584]{1,0:T(8,128)(2,1)}) %all-gather.12.cloned.1.call-update) | async-done | bytes 3670032 | tf_op jit(solution)/shard_map/all_gather | solution.py:52
  285.4 7.4 %fusion.5 = f32[512,1024]{1,0:T(8,128)S(1)} fusion(bf16[512,3584]{1,0:T(8,128)(2,1)} %all-gather.12.cloned.1.call-done, bf16[1024,3584]{1,0:T(8,128)(2,1)} %param.7), kind=kOutput, calls=%fused_computation.15 | convolution fusion | flops 3758096384 | bytes 13107200 | tf_op jit(solution)/shard_map/dot_general | solution.py:8
  292.7 29.4 %all-gather.14.cloned.1.call-done = bf16[512,3584]{1,0:T(8,128)(2,1)} async-done(((bf16[64,3584]{1,0:T(8,128)(2,1)}), bf16[512,3584]{1,0:T(8,128)(2,1)}) %all-gather.14.cloned.1.call-update) | async-done | bytes 3670032 | tf_op jit(solution)/shard_map/all_gather | solution.py:53
  322.1 9.2 %add_convert_fusion = bf16[512,1024]{1,0:T(8,128)(2,1)} fusion(f32[512,1024]{1,0:T(8,128)S(1)} %fusion.5, bf16[512,3584]{1,0:T(8,128)(2,1)} %all-gather.14.cloned.1.call-done, bf16[1024,3584]{1,0:T(8,128)(2,1)} %param.8), kind=kOutput, calls=%fused_computation.6 | convolution fusion | flops 3759144960 | bytes 14155776 | tf_op jit(solution)/shard_map/dot_general | solution.py:8
  331.3 0.0 reduce-scatter.11.cloned.1.call-update
  331.3 0.2 reduce-scatter.7.cloned.1.call-start
  331.6 27.4 %all-gather.8.cloned.1.call-done = bf16[512,3584]{1,0:T(8,128)(2,1)} async-done(((bf16[64,3584]{1,0:T(8,128)(2,1)}), bf16[512,3584]{1,0:T(8,128)(2,1)}) %all-gather.8.cloned.1.call-update) | async-done | bytes 3670032 | tf_op jit(solution)/shard_map/all_gather | solution.py:36
  359.0 9.1 %convolution_convert_fusion.3 = bf16[512,1024]{1,0:T(8,128)(2,1)} fusion(bf16[512,3584]{1,0:T(8,128)(2,1)} %all-gather.8.cloned.1.call-done, bf16[3584,1024]{1,0:T(8,128)(2,1)} %param.9), kind=kOutput, calls=%fused_computation.7 | convolution fusion | flops 3758620672 | bytes 12058624 | tf_op jit(solution)/shard_map/dot_general | solution.py:39
  368.1 0.0 reduce-scatter.7.cloned.1.call-update
  368.1 8.1 %fusion = bf16[1024,3584]{0,1:T(8,128)(2,1)} fusion(bf16[512,3584]{1,0:T(8,128)(2,1)} %all-gather.12.cloned.1.call-done, bf16[512,1024]{1,0:T(8,128)(2,1)S(1)} %copy-done.1), kind=kOutput, calls=%fused_computation.4 | convolution fusion | flops 3761766400 | bytes 12058624 | tf_op jit(solution)/shard_map/dot_general | solution.py:8
  376.2 10.0 %copy.10 = bf16[1024,3584]{1,0:T(8,128)(2,1)} copy(bf16[1024,3584]{0,1:T(8,128)(2,1)} %fusion) | data formatting | bytes 14680064
  386.2 8.1 %fusion.1 = bf16[1024,3584]{0,1:T(8,128)(2,1)} fusion(bf16[512,3584]{1,0:T(8,128)(2,1)} %all-gather.14.cloned.1.call-done, bf16[512,1024]{1,0:T(8,128)(2,1)S(1)} %copy-done.1), kind=kOutput, calls=%fused_computation.5 | convolution fusion | flops 3761766400 | bytes 12058624 | tf_op jit(solution)/shard_map/dot_general | solution.py:8
  394.3 0.0 copy-start
  394.3 10.0 %copy.11 = bf16[1024,3584]{1,0:T(8,128)(2,1)} copy(bf16[1024,3584]{0,1:T(8,128)(2,1)} %fusion.1) | data formatting | bytes 14680064
  404.4 0.0 copy-done
  404.4 8.1 %convolution_convert_fusion = bf16[3584,1024]{1,0:T(8,128)(2,1)} fusion(bf16[512,3584]{1,0:T(8,128)(2,1)} %all-gather.8.cloned.1.call-done, bf16[512,1024]{1,0:T(8,128)(2,1)S(1)} %copy-done), kind=kOutput, calls=%fused_computation.1 | convolution fusion | flops 3761766400 | bytes 12058624 | tf_op jit(solution)/shard_map/dot_general | solution.py:8
  412.5 0.0 reduce-scatter.11.cloned.1.call-done
  412.5 5.4 %reduce-scatter.7.cloned.1.call-done = bf16[128,1024]{1,0:T(8,128)(2,1)} async-done(((bf16[512,1024]{1,0:T(8,128)(2,1)}), bf16[128,1024]{1,0:T(8,128)(2,1)}) %reduce-scatter.7.cloned.1.call-update) | async-done | bytes 262160 | tf_op jit(solution)/shard_map/reduce_scatter | solution.py:38
Async XLA Ops:
  7.2 33.1 %all-gather.10.cloned.1.call-start = ((), (), s32[]{:S(2)}) async-start(), calls=%async_computation.8 | async-start | bytes 1310720 | tf_op jit(solution)/shard_map/all_gather | solution.py:16
  7.9 61.3 %all-gather.6.cloned.1.call-start = ((), (), s32[]{:S(2)}) async-start(), calls=%async_computation.4 | async-start | bytes 1310720 | tf_op jit(solution)/shard_map/all_gather | solution.py:15
  8.6 130.9 %reduce-scatter.9.cloned.1.call-start = ((), (), s32[]{:S(2)}) async-start(), calls=%async_computation.9 | async-start | bytes 8257536 | tf_op jit(solution)/shard_map/reduce_scatter | solution.py:46
  50.8 196.8 %reduce-scatter.5.cloned.1.call-start = ((), (), s32[]{:S(2)}) async-start(), calls=%async_computation.5 | async-start | bytes 16515072 | tf_op jit(solution)/shard_map/reduce_scatter | solution.py:20
  69.2 7.5 %copy-start.1 = (bf16[512,1024]{1,0:T(8,128)(2,1)S(1)}, bf16[512,1024]{1,0:T(8,128)(2,1)}, u32[]{:S(2)}) copy-start(bf16[512,1024]{1,0:T(8,128)(2,1)} %all-gather.6.cloned.1.call-done) | copy-start | bytes 3145732
  89.9 195.5 %all-gather.12.cloned.1.call-start = ((), (), s32[]{:S(2)}) async-start(), calls=%async_computation.10 | async-start | bytes 4128768 | tf_op jit(solution)/shard_map/all_gather | solution.py:52
  250.8 71.3 %all-gather.14.cloned.1.call-start = ((), (), s32[]{:S(2)}) async-start(), calls=%async_computation.11 | async-start | bytes 4128768 | tf_op jit(solution)/shard_map/all_gather | solution.py:53
  251.4 107.6 %all-gather.8.cloned.1.call-start = ((), (), s32[]{:S(2)}) async-start(), calls=%async_computation.6 | async-start | bytes 4128768 | tf_op jit(solution)/shard_map/all_gather | solution.py:36
  252.2 160.3 %reduce-scatter.11.cloned.1.call-start = ((), (), s32[]{:S(2)}) async-start(), calls=%async_computation.12 | async-start | bytes 1310720 | tf_op jit(solution)/shard_map/reduce_scatter | solution.py:57
  331.3 86.5 %reduce-scatter.7.cloned.1.call-start = ((), (), s32[]{:S(2)}) async-start(), calls=%async_computation.7 | async-start | bytes 1310720 | tf_op jit(solution)/shard_map/reduce_scatter | solution.py:38
  394.3 10.1 %copy-start = (bf16[512,1024]{1,0:T(8,128)(2,1)S(1)}, bf16[512,1024]{1,0:T(8,128)(2,1)}, u32[]{:S(2)}) copy-start(bf16[512,1024]{1,0:T(8,128)(2,1)} %all-gather.10.cloned.1.call-done) | copy-start | bytes 3145732
Sparse Core Ops, SparseCore 0:
  9.5 30.6 all-gather.9
  41.8 27.3 all-gather.5
  73.2 66.3 reduce-scatter.8
  142.9 104.5 reduce-scatter.4
  250.9 34.3 all-gather.11
  287.7 34.3 all-gather.13
  324.6 34.3 all-gather.7
  361.8 27.2 reduce-scatter.10
  392.0 25.7 reduce-scatter.6
where the time goes:
time: 425 us; the launch traced here: 424 us
  waiting for transfers between devices  306 us (72%)
  matrix products  74.8 us (18%)
  local copies, waits for them, and re-layouts  20 us (5%)
  between operations  13.9 us (3%)
  other arithmetic  9.61 us (2%)
    reduce_scatter x1, waiting for transfers between devices, per_device(): lax.psum_scatter(jnp.concatenate([jnp.dot(rows, gate_weight, preferred_el...  108 us
    dot_general x6, matrix products, contract(): lax.dot_general(left, right, (((left_dim,), (right_dim,)), ((), ())), pre...  51.4 us
    reduce_scatter x1, waiting for transfers between devices, per_device(): lax.psum_scatter(contract(rows, down_weight, 1, 1), 'dp', scatter_dimensi...  49.6 us
    all_gather x1, waiting for transfers between devices, per_device(): lax.all_gather(d_gate, 'dp', axis=0, tiled=True)  33.2 us
    all_gather x1, waiting for transfers between devices, per_device(): lax.all_gather(cotangent, 'mp', axis=0, tiled=True)  31.6 us
    all_gather x1, waiting for transfers between devices, per_device(): lax.all_gather(d_up, 'dp', axis=0, tiled=True)  29.4 us
    all_gather x1, waiting for transfers between devices, per_device(): all_hidden = lax.all_gather(hidden, 'dp', axis=0, tiled=True)  27.4 us
    unnamed x6, local copies, waits for them, and re-layouts  20 us
  transfers between devices with their start and end apart: 9, of which 8 were waited for; matrix products, arithmetic and copies ran while one was open for 24% of the time, Pallas kernels for 0%

commit v1 on v0

--- a/solution.py
+++ b/solution.py
@@ -33,7 +33,19 @@
     up = stacked[:, columns:]
     sig = jax.nn.sigmoid(gate)
     hidden = (gate * sig * up).astype(jnp.bfloat16)
-    all_hidden = lax.all_gather(hidden, "dp", axis=0, tiled=True)
+
+    def edit_spots(target, d_out):
+        n_parts = lax.axis_size("dp")
+        last = sorted(((c, (c + 1) % n_parts) for c in range(n_parts)))
+        q_next = target
+        all_rows = [q_next]
+        for to_i in tuple(range(1, n_parts)):
+            q_next = lax.ppermute(q_next, axis_name="dp", perm=last)
+            all_rows.insert(0, q_next)
+        built = jnp.concatenate(all_rows, axis=d_out)
+        return jnp.roll(built, (lax.axis_index("dp") + 1) * target.shape[d_out], d_out)
+
+    all_hidden = edit_spots(hidden, 0)
     rows = all_hidden
     output = lax.psum_scatter(
         jnp.dot(rows, down_weight, preferred_element_type=jnp.float32).astype(jnp.bfloat16),

time: 425 us -> 416 us (0.979)
  waiting for transfers between devices: 306 us -> 295 us
  local copies, waits for them, and re-layouts: 20 us -> 25.5 us
    ppermute x0 -> x7, waiting for transfers between devices: none -> 72.2 us  [edit_spots(): q_next = lax.ppermute(q_next, axis_name='dp', perm=last)]
    all_gather x1, waiting for transfers between devices: 33.2 us -> 0.02 us  [per_device(): lax.all_gather(d_gate, 'dp', axis=0, tiled=True)]
    all_gather x1 -> x0, waiting for transfers between devices: 27.4 us -> none  [per_device(): all_hidden = lax.all_gather(hidden, 'dp', axis=0, tiled=True)]
    all_gather x1, waiting for transfers between devices: 29.4 us -> 6.12 us  [per_device(): lax.all_gather(d_up, 'dp', axis=0, tiled=True)]
    reduce_scatter x1, waiting for transfers between devices: 0.01 us -> 7.13 us  [per_device(): lax.psum_scatter((contract(all_d_gate, gate_weight, 1, 1) + contract(all_...]
    unnamed x6 -> x27, local copies, waits for them, and re-layouts: 20 us -> 25.5 us
    reduce_scatter x1, waiting for transfers between devices: 5.36 us -> 0.01 us  [per_device(): lax.psum_scatter(jnp.dot(rows, down_weight, preferred_element_type=jnp.fl...]
  transfers between devices with their start and end apart: 9 -> 15, of which waited for: 8 -> 13; matrix products, arithmetic and copies ran while one was open for 24% -> 24% of each run, Pallas kernels for 0% -> 0%
where the time goes in v1:
time: 416 us
  waiting for transfers between devices  295 us (71%)
  matrix products  71.2 us (17%)
  local copies, waits for them, and re-layouts  25.5 us (6%)
  between operations  14.4 us (3%)
  other arithmetic  9.5 us (2%)
    reduce_scatter x1, waiting for transfers between devices, per_device(): lax.psum_scatter(jnp.concatenate([jnp.dot(rows, gate_weight, preferred_el...  108 us
    ppermute x7, waiting for transfers between devices, edit_spots(): q_next = lax.ppermute(q_next, axis_name='dp', perm=last)  72.2 us
    reduce_scatter x1, waiting for transfers between devices, per_device(): lax.psum_scatter(contract(rows, down_weight, 1, 1), 'dp', scatter_dimensi...  49.6 us
    dot_general x6, matrix products, contract(): lax.dot_general(left, right, (((left_dim,), (right_dim,)), ((), ())), pre...  49.6 us
    all_gather x1, waiting for transfers between devices, per_device(): lax.all_gather(cotangent, 'mp', axis=0, tiled=True)  31.6 us
    unnamed x27, local copies, waits for them, and re-layouts  25.5 us
    all_gather x1, waiting for transfers between devices, per_device(): lax.all_gather(tokens, 'mp', axis=0, tiled=True)  18.4 us
  transfers between devices with their start and end apart: 15, of which 13 were waited for; matrix products, arithmetic and copies ran while one was open for 24% of the time, Pallas kernels for 0%

profile of v1, /device:TPU:0, one launch (start us, length us, event | category | flops | bytes accessed | tf_op | source)
XLA Modules:
  0.0 415.7 jit_solution(14284246303761192209)
XLA Ops:
  7.2 0.0 all-gather.7.cloned.1.call-start
  7.2 0.7 all-gather.7.cloned.1.call-update
  7.9 0.0 all-gather.5.cloned.1.call-start
  7.9 0.7 all-gather.5.cloned.1.call-update
  8.6 0.0 reduce-scatter.9.cloned.1.call-start
  8.7 31.6 %all-gather.7.cloned.1.call-done = bf16[512,1024]{1,0:T(8,128)(2,1)} async-done(((bf16[128,1024]{1,0:T(8,128)(2,1)}), bf16[512,1024]{1,0:T(8,128)(2,1)}) %all-gather.7.cloned.1.call-update) | async-done | bytes 1048592 | tf_op jit(solution)/shard_map/all_gather | solution.py:16
  40.3 10.5 %fusion.12 = f32[512,3584]{1,0:T(8,128)} fusion(bf16[512,1024]{1,0:T(8,128)(2,1)} %all-gather.7.cloned.1.call-done, bf16[3584,1024]{1,0:T(8,128)(2,1)} %param.9), kind=kOutput, calls=%fused_computation.35 | convolution fusion | flops 3758096384 | bytes 15728640 | tf_op jit(solution)/shard_map/dot_general | solution.py:8
  50.7 0.0 reduce-scatter.9.cloned.1.call-update
  50.8 0.0 reduce-scatter.5.cloned.1.call-start
  50.8 18.4 %all-gather.5.cloned.1.call-done = bf16[512,1024]{1,0:T(8,128)(2,1)} async-done(((bf16[128,1024]{1,0:T(8,128)(2,1)}), bf16[512,1024]{1,0:T(8,128)(2,1)}) %all-gather.5.cloned.1.call-update) | async-done | bytes 1048592 | tf_op jit(solution)/shard_map/all_gather | solution.py:15
  69.2 7.4 %fusion.10 = f32[512,3584]{1,0:T(8,128)S(1)} fusion(bf16[512,1024]{1,0:T(8,128)(2,1)} %all-gather.5.cloned.1.call-done, bf16[1024,3584]{1,0:T(8,128)(2,1)} %param.7), kind=kOutput, calls=%fused_computation.33 | convolution fusion | flops 3758096384 | bytes 15728640 | tf_op jit(solution)/shard_map/dot_general | solution.py:23
  76.7 6.8 %fusion.11 = f32[512,3584]{1,0:T(8,128)S(1)} fusion(bf16[512,1024]{1,0:T(8,128)(2,1)S(1)} %copy-done.3, bf16[1024,3584]{1,0:T(8,128)(2,1)} %param.8), kind=kOutput, calls=%fused_computation.34 | convolution fusion | flops 3758096384 | bytes 15728640 | tf_op jit(solution)/shard_map/dot_general | solution.py:24
  83.5 6.4 %pad_maximum_fusion = f32[512,7168]{1,0:T(8,128)} fusion(f32[512,3584]{1,0:T(8,128)S(1)} %fusion.11, f32[512,3584]{1,0:T(8,128)S(1)} %fusion.10), kind=kLoop, calls=%fused_computation | loop fusion | flops 3670016 | bytes 29360128 | tf_op jit(solution)/shard_map/concatenate | solution.py:21
  89.9 0.0 reduce-scatter.5.cloned.1.call-update
  89.9 0.0 all-gather.9.cloned.1.call-start
  90.0 49.6 %reduce-scatter.9.cloned.1.call-done = f32[64,3584]{1,0:T(8,128)} async-done(((f32[512,3584]{1,0:T(8,128)}), f32[64,3584]{1,0:T(8,128)}) %reduce-scatter.9.cloned.1.call-update) | async-done | bytes 917520 | tf_op jit(solution)/shard_map/reduce_scatter | solution.py:58
  139.6 108.0 %reduce-scatter.5.cloned.1.call-done = f32[64,7168]{1,0:T(8,128)} async-done(((f32[512,7168]{1,0:T(8,128)}), f32[64,7168]{1,0:T(8,128)}) %reduce-scatter.5.cloned.1.call-update) | async-done | bytes 1835024 | tf_op jit(solution)/shard_map/reduce_scatter | solution.py:20
  247.6 3.1 multiply_convert_fusion
  250.7 0.0 all-gather.9.cloned.1.call-update
  250.7 0.0 all-gather.11.cloned.1.call-start
  250.8 0.1 collective-permute-start
  250.8 8.8 %collective-permute-done = bf16[64,3584]{1,0:T(8,128)(2,1)S(1)} collective-permute-done((bf16[64,3584]{1,0:T(8,128)(2,1)S(1)}, bf16[64,3584]{1,0:T(8,128)(2,1)S(1)}, u32[]{:S(2)}, u32[]{:S(2)}) %collective-permute-start) | collective-permute-done | bytes 458784 | tf_op jit(solution)/shard_map/ppermute | solution.py:43
  259.6 12.1 %collective-permute-done.1 = bf16[64,3584]{1,0:T(8,128)(2,1)S(1)} collective-permute-done((bf16[64,3584]{1,0:T(8,128)(2,1)S(1)}, bf16[64,3584]{1,0:T(8,128)(2,1)S(1)}, u32[]{:S(2)}, u32[]{:S(2)}) %collective-permute-start.1) | collective-permute-done | bytes 458784 | tf_op jit(solution)/shard_map/ppermute | solution.py:43
  271.8 16.1 %collective-permute-done.2 = bf16[64,3584]{1,0:T(8,128)(2,1)S(1)} collective-permute-done((bf16[64,3584]{1,0:T(8,128)(2,1)S(1)}, bf16[64,3584]{1,0:T(8,128)(2,1)S(1)}, u32[]{:S(2)}, u32[]{:S(2)}) %collective-permute-start.2) | collective-permute-done | bytes 458784 | tf_op jit(solution)/shard_map/ppermute | solution.py:43
  287.8 8.8 %collective-permute-done.3 = bf16[64,3584]{1,0:T(8,128)(2,1)S(1)} collective-permute-done((bf16[64,3584]{1,0:T(8,128)(2,1)S(1)}, bf16[64,3584]{1,0:T(8,128)(2,1)S(1)}, u32[]{:S(2)}, u32[]{:S(2)}) %collective-permute-start.3) | collective-permute-done | bytes 458784 | tf_op jit(solution)/shard_map/ppermute | solution.py:43
  296.6 8.8 %collective-permute-done.4 = bf16[64,3584]{1,0:T(8,128)(2,1)S(1)} collective-permute-done((bf16[64,3584]{1,0:T(8,128)(2,1)S(1)}, bf16[64,3584]{1,0:T(8,128)(2,1)S(1)}, u32[]{:S(2)}, u32[]{:S(2)}) %collective-permute-start.4) | collective-permute-done | bytes 458784 | tf_op jit(solution)/shard_map/ppermute | solution.py:43
  305.4 8.8 %collective-permute-done.5 = bf16[64,3584]{1,0:T(8,128)(2,1)S(1)} collective-permute-done((bf16[64,3584]{1,0:T(8,128)(2,1)S(1)}, bf16[64,3584]{1,0:T(8,128)(2,1)S(1)}, u32[]{:S(2)}, u32[]{:S(2)}) %collective-permute-start.5) | collective-permute-done | bytes 458784 | tf_op jit(solution)/shard_map/ppermute | solution.py:43
  314.3 0.0 all-gather.11.cloned.1.call-update
  314.3 0.0 reduce-scatter.7.cloned.1.call-start
  314.3 8.8 %collective-permute-done.6 = bf16[64,3584]{1,0:T(8,128)(2,1)} collective-permute-done((bf16[64,3584]{1,0:T(8,128)(2,1)S(1)}, bf16[64,3584]{1,0:T(8,128)(2,1)}, u32[]{:S(2)}, u32[]{:S(2)}) %collective-permute-start.6) | collective-permute-done | bytes 458784 | tf_op jit(solution)/shard_map/ppermute | solution.py:43
  323.2 1.1 constant_dynamic-update-slice_fusion.15
  324.5 1.1 constant_dynamic-update-slice_fusion.7
  325.8 0.0 copy-start
  325.8 3.0 copy-done
  328.9 7.3 %fusion.5 = bf16[512,1024]{1,0:T(8,128)(2,1)} fusion(bf16[3584,1024]{1,0:T(8,128)(2,1)} %param.9, bf16[1024,3584]{1,0:T(8,128)(2,1)S(1)} %constant_dynamic-update-slice_fusion, s32[]{:T(128)S(6)} %select_n.14), kind=kOutput, calls=%fused_computation.10 | convolution fusion | flops 3758620672 | bytes 12058628 | tf_op jit(solution)/shard_map/dot_general | solution.py:51
  336.2 0.0 reduce-scatter.7.cloned.1.call-update
  336.3 0.2 reduce-scatter.11.cloned.1.call-start
  336.5 0.0 all-gather.9.cloned.1.call-done
  336.5 7.4 %fusion.13 = f32[512,1024]{1,0:T(8,128)S(1)} fusion(bf16[512,3584]{1,0:T(8,128)(2,1)} %all-gather.9.cloned.1.call-done, bf16[1024,3584]{1,0:T(8,128)(2,1)} %param.7), kind=kOutput, calls=%fused_computation.36 | convolution fusion | flops 3758096384 | bytes 13107200 | tf_op jit(solution)/shard_map/dot_general | solution.py:8
  343.9 6.1 %all-gather.11.cloned.1.call-done = bf16[512,3584]{1,0:T(8,128)(2,1)} async-done(((bf16[64,3584]{1,0:T(8,128)(2,1)}), bf16[512,3584]{1,0:T(8,128)(2,1)}) %all-gather.11.cloned.1.call-update) | async-done | bytes 3670032 | tf_op jit(solution)/shard_map/all_gather | solution.py:65
  350.0 9.2 %add_convert_fusion = bf16[512,1024]{1,0:T(8,128)(2,1)} fusion(f32[512,1024]{1,0:T(8,128)S(1)} %fusion.13, bf16[512,3584]{1,0:T(8,128)(2,1)} %all-gather.11.cloned.1.call-done, bf16[1024,3584]{1,0:T(8,128)(2,1)} %param.8), kind=kOutput, calls=%fused_computation.9 | convolution fusion | flops 3759144960 | bytes 14155776 | tf_op jit(solution)/shard_map/dot_general | solution.py:8
  359.2 0.0 reduce-scatter.11.cloned.1.call-update
  359.3 8.3 %convolution_convert_fusion = bf16[3584,1024]{1,0:T(8,128)(2,1)} fusion(bf16[512,1024]{1,0:T(8,128)(2,1)S(1)} %copy-done.2, bf16[1024,3584]{1,0:T(8,128)(2,1)} %copy-done, s32[]{:T(128)S(6)} %select_n.14), kind=kOutput, calls=%fused_computation.1 | convolution fusion | flops 3761766400 | bytes 12058628 | tf_op jit(solution)/shard_map/dot_general | solution.py:8
  367.6 6.1 %fusion = bf16[1024,3584]{0,1:T(8,128)(2,1)} fusion(bf16[512,3584]{1,0:T(8,128)(2,1)S(1)} %copy-done.1, bf16[512,1024]{1,0:T(8,128)(2,1)S(1)} %copy-done.4), kind=kOutput, calls=%fused_computation.4 | convolution fusion | flops 3761766400 | bytes 12058624 | tf_op jit(solution)/shard_map/dot_general | solution.py:8
  373.7 10.0 %copy.10 = bf16[1024,3584]{1,0:T(8,128)(2,1)} copy(bf16[1024,3584]{0,1:T(8,128)(2,1)} %fusion) | data formatting | bytes 14680064
  383.6 8.2 %fusion.1 = bf16[1024,3584]{0,1:T(8,128)(2,1)} fusion(bf16[512,3584]{1,0:T(8,128)(2,1)} %all-gather.11.cloned.1.call-done, bf16[512,1024]{1,0:T(8,128)(2,1)S(1)} %copy-done.4), kind=kOutput, calls=%fused_computation.5 | convolution fusion | flops 3761766400 | bytes 12058624 | tf_op jit(solution)/shard_map/dot_general | solution.py:8
  391.8 10.0 %copy.11 = bf16[1024,3584]{1,0:T(8,128)(2,1)} copy(bf16[1024,3584]{0,1:T(8,128)(2,1)} %fusion.1) | data formatting | bytes 14680064
  401.8 7.1 %reduce-scatter.11.cloned.1.call-done = bf16[128,1024]{1,0:T(8,128)(2,1)} async-done(((bf16[512,1024]{1,0:T(8,128)(2,1)}), bf16[128,1024]{1,0:T(8,128)(2,1)}) %reduce-scatter.11.cloned.1.call-update) | async-done | bytes 262160 | tf_op jit(solution)/shard_map/reduce_scatter | solution.py:69
  (29 shorter events, 0.5 us)
Async XLA Ops:
  7.2 33.1 %all-gather.7.cloned.1.call-start = ((), (), s32[]{:S(2)}) async-start(), calls=%async_computation.7 | async-start | bytes 1310720 | tf_op jit(solution)/shard_map/all_gather | solution.py:16
  7.9 61.3 %all-gather.5.cloned.1.call-start = ((), (), s32[]{:S(2)}) async-start(), calls=%async_computation.4 | async-start | bytes 1310720 | tf_op jit(solution)/shard_map/all_gather | solution.py:15
  8.6 130.9 %reduce-scatter.9.cloned.1.call-start = ((), (), s32[]{:S(2)}) async-start(), calls=%async_computation.8 | async-start | bytes 8257536 | tf_op jit(solution)/shard_map/reduce_scatter | solution.py:58
  50.8 196.8 %reduce-scatter.5.cloned.1.call-start = ((), (), s32[]{:S(2)}) async-start(), calls=%async_computation.5 | async-start | bytes 16515072 | tf_op jit(solution)/shard_map/reduce_scatter | solution.py:20
  69.2 7.5 %copy-start.3 = (bf16[512,1024]{1,0:T(8,128)(2,1)S(1)}, bf16[512,1024]{1,0:T(8,128)(2,1)}, u32[]{:S(2)}) copy-start(bf16[512,1024]{1,0:T(8,128)(2,1)} %all-gather.5.cloned.1.call-done) | copy-start | bytes 3145732
  89.9 246.6 %all-gather.9.cloned.1.call-start = ((), (), s32[]{:S(2)}) async-start(), calls=%async_computation.9 | async-start | bytes 4128768 | tf_op jit(solution)/shard_map/all_gather | solution.py:64
  250.7 99.3 %all-gather.11.cloned.1.call-start = ((), (), s32[]{:S(2)}) async-start(), calls=%async_computation.10 | async-start | bytes 4128768 | tf_op jit(solution)/shard_map/all_gather | solution.py:65
  250.8 8.9 %collective-permute-start = (bf16[64,3584]{1,0:T(8,128)(2,1)S(1)}, bf16[64,3584]{1,0:T(8,128)(2,1)S(1)}, u32[]{:S(2)}, u32[]{:S(2)}) collective-permute-start(bf16[64,3584]{1,0:T(8,128)(2,1)S(1)} %get-tuple-element.12), channel_id=1, source_target_pairs={{0,4},{4,8},{8,12},{12,16},{16,20},{20,24},{24,28},{28,0},{1,5},{5... | collective-permute-start | bytes 1376264 | tf_op jit(solution)/shard_map/ppermute | solution.py:43
  259.6 12.1 %collective-permute-start.1 = (bf16[64,3584]{1,0:T(8,128)(2,1)S(1)}, bf16[64,3584]{1,0:T(8,128)(2,1)S(1)}, u32[]{:S(2)}, u32[]{:S(2)}) collective-permute-start(bf16[64,3584]{1,0:T(8,128)(2,1)S(1)} %collective-permute-done), channel_id=1, source_target_pairs={{0,4},{4,8},{8,12},{12,16},{16,20},{20,24},{24,28},{28,0},{1,5},{5... | collective-permute-start | bytes 1376264 | tf_op jit(solution)/shard_map/ppermute | solution.py:43
  271.8 16.1 %collective-permute-start.2 = (bf16[64,3584]{1,0:T(8,128)(2,1)S(1)}, bf16[64,3584]{1,0:T(8,128)(2,1)S(1)}, u32[]{:S(2)}, u32[]{:S(2)}) collective-permute-start(bf16[64,3584]{1,0:T(8,128)(2,1)S(1)} %collective-permute-done.1), channel_id=1, source_target_pairs={{0,4},{4,8},{8,12},{12,16},{16,20},{20,24},{24,28},{28,0},{1,5},{5... | collective-permute-start | bytes 1376264 | tf_op jit(solution)/shard_map/ppermute | solution.py:43
  287.8 8.8 %collective-permute-start.3 = (bf16[64,3584]{1,0:T(8,128)(2,1)S(1)}, bf16[64,3584]{1,0:T(8,128)(2,1)S(1)}, u32[]{:S(2)}, u32[]{:S(2)}) collective-permute-start(bf16[64,3584]{1,0:T(8,128)(2,1)S(1)} %collective-permute-done.2), channel_id=1, source_target_pairs={{0,4},{4,8},{8,12},{12,16},{16,20},{20,24},{24,28},{28,0},{1,5},{5... | collective-permute-start | bytes 1376264 | tf_op jit(solution)/shard_map/ppermute | solution.py:43
  296.6 8.8 %collective-permute-start.4 = (bf16[64,3584]{1,0:T(8,128)(2,1)S(1)}, bf16[64,3584]{1,0:T(8,128)(2,1)S(1)}, u32[]{:S(2)}, u32[]{:S(2)}) collective-permute-start(bf16[64,3584]{1,0:T(8,128)(2,1)S(1)} %collective-permute-done.3), channel_id=1, source_target_pairs={{0,4},{4,8},{8,12},{12,16},{16,20},{20,24},{24,28},{28,0},{1,5},{5... | collective-permute-start | bytes 1376264 | tf_op jit(solution)/shard_map/ppermute | solution.py:43
  305.4 8.8 %collective-permute-start.5 = (bf16[64,3584]{1,0:T(8,128)(2,1)S(1)}, bf16[64,3584]{1,0:T(8,128)(2,1)S(1)}, u32[]{:S(2)}, u32[]{:S(2)}) collective-permute-start(bf16[64,3584]{1,0:T(8,128)(2,1)S(1)} %collective-permute-done.4), channel_id=1, source_target_pairs={{0,4},{4,8},{8,12},{12,16},{16,20},{20,24},{24,28},{28,0},{1,5},{5... | collective-permute-start | bytes 1376264 | tf_op jit(solution)/shard_map/ppermute | solution.py:43
  314.2 8.9 %collective-permute-start.6 = (bf16[64,3584]{1,0:T(8,128)(2,1)S(1)}, bf16[64,3584]{1,0:T(8,128)(2,1)}, u32[]{:S(2)}, u32[]{:S(2)}) collective-permute-start(bf16[64,3584]{1,0:T(8,128)(2,1)S(1)} %collective-permute-done.5), channel_id=1, source_target_pairs={{0,4},{4,8},{8,12},{12,16},{16,20},{20,24},{24,28},{28,0},{1,5},{5... | collective-permute-start | bytes 1376264 | tf_op jit(solution)/shard_map/ppermute | solution.py:43
  314.3 87.5 %reduce-scatter.7.cloned.1.call-start = ((), (), s32[]{:S(2)}) async-start(), calls=%async_computation.6 | async-start | bytes 1310720 | tf_op jit(solution)/shard_map/reduce_scatter | solution.py:50
  325.8 3.1 copy-start
  336.3 72.6 %reduce-scatter.11.cloned.1.call-start = ((), (), s32[]{:S(2)}) async-start(), calls=%async_computation.11 | async-start | bytes 1310720 | tf_op jit(solution)/shard_map/reduce_scatter | solution.py:69
  343.9 15.4 %copy-start.2 = (bf16[512,1024]{1,0:T(8,128)(2,1)S(1)}, bf16[512,1024]{1,0:T(8,128)(2,1)}, u32[]{:S(2)}) copy-start(bf16[512,1024]{1,0:T(8,128)(2,1)} %all-gather.7.cloned.1.call-done) | copy-start | bytes 3145732
  359.3 8.3 %copy-start.1 = (bf16[512,3584]{1,0:T(8,128)(2,1)S(1)}, bf16[512,3584]{1,0:T(8,128)(2,1)}, u32[]{:S(2)}) copy-start(bf16[512,3584]{1,0:T(8,128)(2,1)} %all-gather.9.cloned.1.call-done) | copy-start | bytes 11010052
  359.3 8.3 %copy-start.4 = (bf16[512,1024]{1,0:T(8,128)(2,1)S(1)}, bf16[512,1024]{1,0:T(8,128)(2,1)}, u32[]{:S(2)}) copy-start(bf16[512,1024]{1,0:T(8,128)(2,1)} %all-gather.5.cloned.1.call-done) | copy-start | bytes 3145732
Sparse Core Ops, SparseCore 0:
  9.5 30.6 all-gather.6
  41.8 27.3 all-gather.4
  73.2 66.3 reduce-scatter.8
  142.9 104.5 reduce-scatter.4
  250.8 41.1 all-gather.8
  314.4 35.5 all-gather.10
  352.9 27.2 reduce-scatter.6
  383.1 25.7 reduce-scatter.10
